TPU v7x, 32 devices: a whole 2x2x4 slice. The times are simulated.
32 devices in a mesh: groups: 2 (over y), heads: 4 (over z), batch: 4 (over x, core).
Axes of the slice: x: 2, y: 2, z: 4, core: 2. Of those that a mesh axis runs over, the one named last changes fastest.
Arguments:
- queries: bfloat16 [128, 8192], P(('groups', 'batch'), 'heads'), parts along dimension 0, may hold values from -110 to 110
- new_kv: bfloat16 [16, 64, 256], P(('groups', 'heads'), 'batch'), parts along dimension 0, may hold values from -15 to 15
- kv_pool: bfloat16 [16, 192, 128, 256], P(('groups', 'heads'), 'batch'), parts along dimension 0, may hold values from -6 to 6
- page_counts: int32 [8, 16], P(('groups', 'batch')), parts along dimension 0, may hold values from 1 to 6, 48 in all within a row
- last_fill: int32 [8, 16], P(('groups', 'batch')), parts along dimension 0, may hold values from 1 to 128
- page_order: int32 [8, 48], P(('groups', 'batch')), parts along dimension 0, may hold values from 0 to 47, each once within a row
- hidden: bfloat16 [128, 8192], P(('groups', 'batch')), parts along dimension 0, may hold values from -0.59765625 to 0.59765625
- out_weight: bfloat16 [8192, 8192], P('heads'), may hold values from -0.5 to 0.5
- norm_gain: bfloat16 [8192], replicated, may hold values from 0.099609375 to 1.8984375
- sectioned: bfloat16 [8, 4, 8, 128, 256], P(('groups', 'heads'), 'batch'), parts along dimension 0, may hold values from -6 to 6
- routes: int32 [8, 4, 8, 1], P(('groups', 'heads'), 'batch'), parts along dimension 0, may hold values from 0 to 7; in each aligned block of 8 rows (0 to 7, 8 to 15, ..., all dimensions but the last counted through in order) at most 2 rows name the same one
Outputs:
- residual_out: bfloat16 [128, 8192], P(('groups', 'batch')), parts along dimension 0
- normed: bfloat16 [128, 8192], P(('groups', 'batch')), parts along dimension 0
- arrival: bfloat16 [16, 4, 4, 2, 128, 256], P(('groups', 'heads'), 'batch'), parts along dimension 0
There are 2 independent parts, one for each index of `groups`. A program takes and returns all parts, laid end to end along the dimension named above; an argument that names none is the same for every part. Nothing has to cross between parts.
Inputs may be any that keep to these rules, and one draw needn't show every extreme that they name: `routes`: every key-value head is named by at most 2 sectioned pages of one device. `page_counts`: the page counts of one batch owner sum to 48.
All inputs are finite; a program needn't handle non-finite values.
Results may differ from a plain program's by a relative error of at most 0.0066.
Values may be sent and summed in bfloat16 or wider, within the bound.
A program may use at most 128 MiB of HBM per device.

v0:
```python
import jax
import jax.numpy as jnp
from jax import lax
from jax.sharding import PartitionSpec as P

KV_HEADS = 8
PER_HEAD_CAP = 2
norm_epsilon = 1e-06


def attend(queries, new_kv, kv_pool, counts, fill, order):
    slot_count, pool_pages, page_size, lane_width = kv_pool.shape
    head_dim = lane_width // 2
    requests = queries.shape[0]
    score_scale = 1.0 / head_dim**0.5
    position = jnp.arange(pool_pages, dtype=jnp.int32)
    position_in_order = jnp.sum(
        jnp.where(order[None, :] == position[:, None], position[None, :], 0), axis=1
    )
    count_ends = jnp.cumsum(counts)
    starts = count_ends - counts
    owner_index = jnp.sum(
        (count_ends[None, :] <= position_in_order[:, None]).astype(jnp.int32), axis=1
    )
    member = owner_index[:, None] == jnp.arange(requests, dtype=jnp.int32)[None, :]
    member_float = member.astype(jnp.float32)
    within = position_in_order - jnp.sum(jnp.where(member, starts[None, :], 0), axis=1)
    context = (counts - 1) * page_size + fill
    context_limit = jnp.sum(jnp.where(member, context[None, :], 0), axis=1)
    live_tokens = (
        within[:, None] * page_size + jnp.arange(page_size, dtype=jnp.int32)[None, :]
        < context_limit[:, None]
    )
    page_queries = jnp.einsum(
        "pr,rlgd->lpgd", member.astype(jnp.bfloat16), queries, preferred_element_type=jnp.float32
    ).astype(jnp.bfloat16)
    scores = (
        jnp.einsum(
            "lpgd,lptd->lpgt",
            page_queries,
            kv_pool[..., :head_dim],
            preferred_element_type=jnp.float32,
        )
        * score_scale
    )
    scores = jnp.where(live_tokens[None, :, None, :], scores, -1e30)
    page_top = jnp.max(scores, axis=3)
    fresh_score = (
        jnp.einsum(
            "rlgd,lrd->lrg", queries, new_kv[..., :head_dim], preferred_element_type=jnp.float32
        )
        * score_scale
    )
    masked_top = jnp.where(member.T[None, :, :, None], page_top[:, None, :, :], -1e30)
    request_top = jnp.maximum(fresh_score, jnp.max(masked_top, axis=2))
    page_ref = jnp.einsum("pr,lrg->lpg", member_float, request_top, precision=lax.Precision.HIGHEST)
    weight = jnp.where(live_tokens[None, :, None, :], jnp.exp(scores - page_ref[..., None]), 0.0)
    page_den = jnp.sum(weight, axis=3)
    page_num = jnp.einsum(
        "lpgt,lptd->lpgd",
        weight.astype(jnp.bfloat16),
        kv_pool[..., head_dim:],
        preferred_element_type=jnp.float32,
    )
    fresh_weight = jnp.exp(fresh_score - request_top)
    fresh_rounded = lax.optimization_barrier(fresh_weight.astype(jnp.bfloat16)).astype(jnp.float32)
    denominator = (
        jnp.einsum("pr,lpg->lrg", member_float, page_den, precision=lax.Precision.HIGHEST)
        + fresh_weight
    )
    numerator = jnp.einsum("pr,lpgd->lrgd", member_float, page_num, precision=lax.Precision.HIGHEST)
    numerator = numerator + fresh_rounded[..., None] * new_kv[:, :, None, head_dim:].astype(
        jnp.float32
    )
    attended = numerator / denominator[..., None]
    attended = jnp.transpose(attended, (1, 0, 2, 3)).astype(jnp.bfloat16)
    return attended.reshape(requests, -1)


def landing_table(destination, head_total, most_pages):
    sectioned_count = destination.shape[0]
    order_ids = jnp.arange(sectioned_count, dtype=jnp.int32)
    same_head = destination[:, None] == destination[None, :]
    earlier = order_ids[:, None] > order_ids[None, :]
    page_rank = jnp.sum((same_head & earlier).astype(jnp.int32), axis=1)
    matches = (
        destination[None, None, :] == jnp.arange(head_total, dtype=jnp.int32)[:, None, None]
    ) & (page_rank[None, None, :] == jnp.arange(most_pages, dtype=jnp.int32)[None, :, None])
    source_index = jnp.sum(jnp.where(matches, order_ids[None, None, :], 0), axis=2)
    source_valid = jnp.any(matches, axis=2)
    return (source_index, source_valid)


def per_device(
    queries,
    new_kv,
    kv_pool,
    page_counts,
    last_fill,
    page_order,
    hidden,
    out_weight,
    norm_gain,
    sectioned,
    routes,
):
    head_count = lax.axis_size("heads")
    slots_dev = new_kv.shape[0]
    head_dim = kv_pool.shape[3] // 2
    requests = hidden.shape[0]
    group_size = queries.shape[1] // (slots_dev * head_dim)
    page_data = sectioned[0, 0]
    source_index, source_valid = landing_table(routes[0, 0, :, 0], KV_HEADS, PER_HEAD_CAP)
    cache_total = head_count * slots_dev
    target = (
        (
            jnp.arange(head_count, dtype=jnp.int32)[None, :] * slots_dev
            + jnp.arange(slots_dev, dtype=jnp.int32)[:, None]
        )
        * KV_HEADS
        // cache_total
    )
    picked = source_index[target]
    present = source_valid[target]
    outgoing = page_data[picked]
    outgoing = jnp.where(present[..., None, None], outgoing, jnp.zeros_like(outgoing))
    landed = lax.all_to_all(outgoing, "heads", split_axis=1, concat_axis=1, tiled=True)
    arrival = landed[:, None]
    query_block = queries.reshape(requests, slots_dev, group_size, head_dim)
    attn = attend(query_block, new_kv, kv_pool, page_counts[0], last_fill[0], page_order[0])
    partial_terms = jnp.dot(attn, out_weight, preferred_element_type=jnp.float32)
    summed = lax.psum(partial_terms, "heads")
    mixed = hidden.astype(jnp.float32) + summed
    mean_square = jnp.mean(mixed * mixed, axis=1, keepdims=True)
    normed = (mixed * lax.rsqrt(mean_square + norm_epsilon) * norm_gain.astype(jnp.float32)).astype(
        jnp.bfloat16
    )
    residual_out = mixed.astype(jnp.bfloat16)
    return (residual_out, normed, arrival)


def solution(mesh):
    return jax.shard_map(
        per_device,
        mesh=mesh,
        in_specs=(
            P(("groups", "batch"), "heads"),
            P(("groups", "heads"), "batch", None),
            P(("groups", "heads"), "batch", None, None),
            P(("groups", "batch"), None),
            P(("groups", "batch"), None),
            P(("groups", "batch"), None),
            P(("groups", "batch"), None),
            P("heads", None),
            P(),
            P(("groups", "heads"), "batch", None, None, None),
            P(("groups", "heads"), "batch", None, None),
        ),
        out_specs=(
            P(("groups", "batch"), None),
            P(("groups", "batch"), None),
            P(("groups", "heads"), "batch", None, None, None, None),
        ),
        check_vma=False,
    )
```

profile of v0, /device:TPU:0, one launch (start us, length us, event | category | flops | bytes accessed | tf_op | source)
XLA Modules:
  0.0 96.6 jit_solution(1213633889777169506)
XLA Ops:
  7.2 0.0 copy-start
  7.2 0.0 all-reduce.2.cloned.1.call-start
  7.2 0.8 select_reduce_fusion.1
  8.0 0.7 copy.69
  8.8 0.1 reduce
  8.9 0.1 convert_reduce_fusion
  9.0 0.7 add_bitcast_fusion
  9.7 0.1 select_reduce_fusion.3
  9.8 0.7 convert_bitcast_fusion
  10.5 0.8 copy.93
  11.4 0.3 fusion.10
  11.6 0.1 fusion.27
  11.8 0.1 copy.90
  11.9 0.1 add_compare_fusion
  12.0 3.7 %fusion.48 = (f32[2,48,8]{2,1,0:T(8,128)S(1)}, f32[2,48,8,128]{3,2,1,0:T(8,128)S(1)}) fusion(bf16[2,48,128,256]{3,2,1,0:T(8,128)(2,1)} %param.13, bf16[2,48,8,128]{3,1,2,0:T(8,128)(2,1)S(1)} %fusion.10, pred[48,128]{1,0:T(8,128)(4,1)S(1)} %add_compare_fusion), kind=kOutput, calls=%fused_computation.86 | convolution fusion | flops 25459968 | bytes 3744768 | tf_op jit(solution)/shard_map/lpgd,lptd->lpgt/dot_general | solution.py:38
  15.7 0.1 copy.72
  15.7 0.1 select_reduce_fusion
  15.9 0.1 copy.73
  15.9 0.1 convolution_bitcast_fusion.1
  16.1 0.1 copy.74
  16.2 0.3 fusion.15
  16.5 2.9 %fusion = f32[2,48,8,128]{3,2,1,0:T(8,128)S(1)} fusion(bf16[2,48,128,256]{3,2,1,0:T(8,128)(2,1)} %param.13, f32[2,48,8,128]{3,2,1,0:T(8,128)S(1)} %get-tuple-element.24, f32[2,48,8]{2,1,0:T(8,128)S(1)} %copy.74, pred[48,128]{1,0:T(8,128)(4,1)S(1)} %add_compare_fusion), kind=kOutput, calls=%fused_computation.3 | convolution fusion | flops 25460736 | bytes 3941376 | tf_op jit(solution)/shard_map/lpgt,lptd->lpgd/dot_general | solution.py:59
  19.3 0.1 copy.76
  19.4 0.1 fusion.13
  19.6 0.3 fusion.12
  19.9 0.0 copy-start.3
  19.9 13.7 %fusion.23 = f32[16,8192]{1,0:T(8,128)} fusion(bf16[2048,8192]{1,0:T(8,128)(2,1)} %param.18, bf16[2,8,16,128]{3,2,1,0:T(8,128)(2,1)S(1)} %bitcast.73), kind=kOutput, calls=%fused_computation.31 | convolution fusion | flops 536870912 | bytes 34144256 | tf_op jit(solution)/shard_map/dot_general | solution.py:131
  33.6 0.0 copy-start.2
  33.6 0.0 copy-start.1
  33.6 0.0 all-reduce.2.cloned.1.call-update
  33.6 0.0 copy-done.3
  33.6 0.2 convert_reduce_fusion.1
  33.8 0.1 and_reduce_fusion
  34.0 0.2 fusion.30
  34.2 0.1 reshape.257
  34.2 0.1 copy.79
  34.3 0.1 copy.82
  34.4 0.6 gather_fusion.1
  35.0 0.6 gather_fusion
  35.6 0.1 copy.92
  35.7 0.1 copy.84
  35.8 0.1 reshape.273
  35.9 0.0 copy-done
  35.9 0.6 gather_fusion.2
  36.5 0.1 broadcast_select_fusion
  36.6 1.1 %copy.85 = bf16[2,4,2,128,256]{4,3,2,0,1:T(8,128)(2,1)} copy(bf16[2,4,2,128,256]{4,3,2,1,0:T(8,128)(2,1)S(1)} %broadcast_select_fusion) | data formatting | bytes 2097152 | tf_op jit(solution)/shard_map/jit(_where)/select_n | solution.py:126
  37.7 6.3 %all-to-all-start = ((bf16[2,4,2,128,256]{4,3,2,0,1:T(8,128)(2,1)}), bf16[2,4,2,128,256]{4,3,2,0,1:T(8,128)(2,1)S(1)}, u32[]{:S(2)}, u32[]{:S(2)}) async-start(bf16[2,4,2,128,256]{4,3,2,0,1:T(8,128)(2,1)} %copy.85), calls=%async_computation | async-start | bytes 2097152 | tf_op jit(solution)/shard_map/all_to_all | solution.py:127
  44.0 0.0 copy-done.2
  44.1 41.5 %all-reduce.2.cloned.1.call-done = f32[16,8192]{1,0:T(8,128)} async-done(((f32[16,8192]{1,0:T(8,128)}), f32[16,8192]{1,0:T(8,128)}) %all-reduce.2.cloned.1.call-update) | async-done | bytes 524304 | tf_op jit(solution)/shard_map/psum | solution.py:132
  85.6 0.0 copy-done.1
  85.6 1.2 %multiply_reduce_fusion = f32[16]{0:T(128)S(1)} fusion(f32[16,8192]{1,0:T(8,128)} %all-reduce.2.cloned.1.call-done, bf16[16,8192]{1,0:T(8,128)(2,1)S(1)} %copy-done.1), kind=kLoop, calls=%fused_computation.19 | loop fusion | flops 524272 | bytes 786496 | tf_op jit(solution)/shard_map/reduce_sum | solution.py:134
  86.8 1.9 %multiply_convert_fusion = (bf16[16,8192]{1,0:T(8,128)(2,1)}, bf16[16,8192]{1,0:T(8,128)(2,1)}) fusion(f32[8192]{0:T(1024)S(1)} %convert_element_type.46, f32[16]{0:T(128)S(1)} %add_rsqrt_fusion, f32[16,8192]{1,0:T(8,128)} %all-reduce.2.cloned.1.call-done, bf16[16,8192]{1,0:T(8,128)(2,1)S(1)} %copy-done.1), kind=kLoop, calls=%fused_computation.18 | loop fusion | flops 786432 | bytes 1343552 | tf_op jit(solution)/shard_map/convert_element_type | solution.py:135
  88.7 0.0 all-to-all-done
  88.7 1.0 %copy.86 = bf16[2,1,4,2,128,256]{5,4,3,2,1,0:T(8,128)(2,1)} copy(bf16[2,1,4,2,128,256]{5,4,3,0,2,1:T(8,128)(2,1)S(1)} %bitcast.71) | data formatting | bytes 2097152
  (15 shorter events, 0.1 us)
Async XLA Ops:
  7.2 28.7 %copy-start = (bf16[1,1,8,128,256]{4,3,2,1,0:T(8,128)(2,1)S(1)}, bf16[1,1,8,128,256]{4,3,2,1,0:T(8,128)(2,1)}, u32[]{:S(2)}) copy-start(bf16[1,1,8,128,256]{4,3,2,1,0:T(8,128)(2,1)} %param.20) | copy-start | bytes 1572868
  7.2 78.4 %all-reduce.2.cloned.1.call-start = ((), (), s32[]{:S(2)}) async-start(), calls=%async_computation.1 | async-start | bytes 1048576 | tf_op jit(solution)/shard_map/psum | solution.py:132
  19.9 13.7 %copy-start.3 = (s32[1,1,8,1]{2,3,1,0:T(1,128)S(1)}, s32[1,1,8,1]{2,3,1,0:T(1,128)}, u32[]{:S(2)}) copy-start(s32[1,1,8,1]{2,3,1,0:T(1,128)} %param.21) | copy-start | bytes 100
  33.6 10.5 %copy-start.2 = (bf16[8192]{0:T(1024)(128)(2,1)S(1)}, bf16[8192]{0:T(1024)(128)(2,1)}, u32[]{:S(2)}) copy-start(bf16[8192]{0:T(1024)(128)(2,1)} %param.19) | copy-start | bytes 49156
  33.6 52.0 %copy-start.1 = (bf16[16,8192]{1,0:T(8,128)(2,1)S(1)}, bf16[16,8192]{1,0:T(8,128)(2,1)}, u32[]{:S(2)}) copy-start(bf16[16,8192]{1,0:T(8,128)(2,1)} %param.17) | copy-start | bytes 786436
  37.7 51.0 %all-to-all-start = ((bf16[2,4,2,128,256]{4,3,2,0,1:T(8,128)(2,1)}), bf16[2,4,2,128,256]{4,3,2,0,1:T(8,128)(2,1)S(1)}, u32[]{:S(2)}, u32[]{:S(2)}) async-start(bf16[2,4,2,128,256]{4,3,2,0,1:T(8,128)(2,1)} %copy.85), calls=%async_computation | async-start | bytes 2097152 | tf_op jit(solution)/shard_map/all_to_all | solution.py:127
Sparse Core Ops, SparseCore 0:
  33.7 51.7 all-reduce.1
where the time goes:
time: 97.1 us; the launch traced here: 96.6 us
  waiting for transfers between devices  41.5 us (43%)
  matrix products  21.2 us (22%)
  between operations  14.2 us (15%)
  other arithmetic  6.9 us (7%)
  local copies, waits for them, and re-layouts  6.39 us (7%)
  starting transfers between devices  6.38 us (7%)
    psum x1, waiting for transfers between devices, per_device(): summed = lax.psum(partial_terms, 'heads')  41.5 us
    dot_general x1, matrix products, per_device(): jnp.dot(attn, out_weight, preferred_element_type=jnp.float32)  13.7 us
    all_to_all x1, starting transfers between devices, per_device(): lax.all_to_all(outgoing, 'heads', split_axis=1, concat_axis=1, tiled=True)  6.35 us
    dot_general x1, matrix products, attend(): jnp.einsum('lpgd,lptd->lpgt', page_queries, kv_pool[..., :head_dim], pref...  3.69 us
    dot_general x1, matrix products, attend(): jnp.einsum('lpgt,lptd->lpgd', weight.astype(jnp.bfloat16), kv_pool[..., h...  2.86 us
  transfers between devices with their start and end apart: 2, of which 1 were waited for; matrix products, arithmetic and copies ran while one was open for 7% of the time, Pallas kernels for 0%

commit v1 on v0

--- a/solution.py
+++ b/solution.py
@@ -129,7 +129,8 @@
     query_block = queries.reshape(requests, slots_dev, group_size, head_dim)
     attn = attend(query_block, new_kv, kv_pool, page_counts[0], last_fill[0], page_order[0])
     partial_terms = jnp.dot(attn, out_weight, preferred_element_type=jnp.float32)
-    summed = lax.psum(partial_terms, "heads")
+    terms = lax.all_gather(partial_terms, "heads")
+    summed = jnp.sum(terms, axis=0)
     mixed = hidden.astype(jnp.float32) + summed
     mean_square = jnp.mean(mixed * mixed, axis=1, keepdims=True)
     normed = (mixed * lax.rsqrt(mean_square + norm_epsilon) * norm_gain.astype(jnp.float32)).astype(

time: 97.1 us -> 114 us (1.17)
  waiting for transfers between devices: 41.5 us -> 58.8 us
    all_to_all x1, waiting for transfers between devices: 0.01 us -> 52.5 us  [per_device(): lax.all_to_all(outgoing, 'heads', split_axis=1, concat_axis=1, tiled=True)]
    psum x1 -> x0, waiting for transfers between devices: 41.5 us -> none  [per_device(): summed = lax.psum(partial_terms, 'heads')]
    all_gather x0 -> x1, waiting for transfers between devices: none -> 6.31 us  [per_device(): terms = lax.all_gather(partial_terms, 'heads')]
    reduce_sum x0 -> x1, other arithmetic: none -> 1.76 us  [per_device(): summed = jnp.sum(terms, axis=0)]
  transfers between devices with their start and end apart: 2 -> 2, of which waited for: 1 -> 2; matrix products, arithmetic and copies ran while one was open for 7% -> 4% of each run, Pallas kernels for 0% -> 0%
where the time goes in v1:
time: 114 us
  waiting for transfers between devices  58.8 us (52%)
  matrix products  21.2 us (19%)
  between operations  14.2 us (12%)
  other arithmetic  6.55 us (6%)
  local copies, waits for them, and re-layouts  6.45 us (6%)
  starting transfers between devices  6.38 us (6%)
    all_to_all x1, waiting for transfers between devices, per_device(): lax.all_to_all(outgoing, 'heads', split_axis=1, concat_axis=1, tiled=True)  52.5 us
    dot_general x1, matrix products, per_device(): jnp.dot(attn, out_weight, preferred_element_type=jnp.float32)  13.7 us
    all_to_all x1, starting transfers between devices, per_device(): lax.all_to_all(outgoing, 'heads', split_axis=1, concat_axis=1, tiled=True)  6.35 us
    all_gather x1, waiting for transfers between devices, per_device(): terms = lax.all_gather(partial_terms, 'heads')  6.31 us
    dot_general x1, matrix products, attend(): jnp.einsum('lpgd,lptd->lpgt', page_queries, kv_pool[..., :head_dim], pref...  3.69 us
    dot_general x1, matrix products, attend(): jnp.einsum('lpgt,lptd->lpgd', weight.astype(jnp.bfloat16), kv_pool[..., h...  2.86 us
  transfers between devices with their start and end apart: 2, of which 2 were waited for; matrix products, arithmetic and copies ran while one was open for 4% of the time, Pallas kernels for 0%

profile of v1, /device:TPU:0, one launch (start us, length us, event | category | flops | bytes accessed | tf_op | source)
XLA Modules:
  0.0 113.6 jit_solution(872474187472810435)
XLA Ops:
  7.2 0.0 copy-start
  7.2 0.0 all-gather.3.cloned.1.call-start
  7.2 0.8 copy.69
  8.0 0.1 reduce
  8.2 0.8 select_reduce_fusion.1
  8.9 0.1 convert_reduce_fusion
  9.0 0.7 add_bitcast_fusion
  9.7 0.1 select_reduce_fusion.3
  9.8 0.9 copy.93
  10.7 0.3 fusion.10
  10.9 0.1 add_compare_fusion
  11.0 3.7 %fusion.48 = (f32[2,48,8]{2,1,0:T(8,128)S(1)}, f32[2,48,8,128]{3,2,1,0:T(8,128)S(1)}) fusion(bf16[2,48,128,256]{3,2,1,0:T(8,128)(2,1)} %param.13, bf16[2,48,8,128]{3,1,2,0:T(8,128)(2,1)S(1)} %fusion.10, pred[48,128]{1,0:T(8,128)(4,1)S(1)} %add_compare_fusion), kind=kOutput, calls=%fused_computation.86 | convolution fusion | flops 25459968 | bytes 3744768 | tf_op jit(solution)/shard_map/lpgd,lptd->lpgt/dot_general | solution.py:38
  14.7 0.1 copy.72
  14.8 0.1 select_reduce_fusion
  14.9 0.1 copy.73
  15.0 0.7 convert_bitcast_fusion
  15.7 0.1 fusion.27
  15.8 0.1 copy.90
  15.9 0.1 convolution_bitcast_fusion.1
  16.0 0.1 copy.74
  16.2 0.3 fusion.15
  16.5 2.9 %fusion = f32[2,48,8,128]{3,2,1,0:T(8,128)S(1)} fusion(bf16[2,48,128,256]{3,2,1,0:T(8,128)(2,1)} %param.13, f32[2,48,8,128]{3,2,1,0:T(8,128)S(1)} %get-tuple-element.24, f32[2,48,8]{2,1,0:T(8,128)S(1)} %copy.74, pred[48,128]{1,0:T(8,128)(4,1)S(1)} %add_compare_fusion), kind=kOutput, calls=%fused_computation.3 | convolution fusion | flops 25460736 | bytes 3941376 | tf_op jit(solution)/shard_map/lpgt,lptd->lpgd/dot_general | solution.py:59
  19.4 0.1 copy.76
  19.4 0.1 fusion.13
  19.6 0.3 fusion.12
  19.9 0.0 copy-start.3
  19.9 13.7 %fusion.23 = f32[16,8192]{1,0:T(8,128)} fusion(bf16[2048,8192]{1,0:T(8,128)(2,1)} %param.18, bf16[2,8,16,128]{3,2,1,0:T(8,128)(2,1)S(1)} %bitcast.75), kind=kOutput, calls=%fused_computation.31 | convolution fusion | flops 536870912 | bytes 34144256 | tf_op jit(solution)/shard_map/dot_general | solution.py:131
  33.6 0.0 copy-start.2
  33.6 0.0 all-gather.3.cloned.1.call-update
  33.6 0.0 copy-done.3
  33.6 0.2 convert_reduce_fusion.1
  33.8 0.1 fusion.30
  34.0 0.1 copy.82
  34.1 0.1 reshape.257
  34.2 0.6 gather_fusion.1
  34.7 0.1 copy.92
  34.8 0.1 copy.84
  34.9 0.1 reshape.273
  35.0 0.1 and_reduce_fusion
  35.2 0.1 copy.79
  35.3 0.6 gather_fusion
  35.9 0.0 copy-done
  35.9 0.0 copy-start.1
  35.9 0.6 gather_fusion.2
  36.5 0.1 broadcast_select_fusion
  36.6 1.1 copy.85
  37.7 6.3 %all-to-all-start = ((bf16[2,4,2,128,256]{4,3,2,0,1:T(8,128)(2,1)}), bf16[2,4,2,128,256]{4,3,2,0,1:T(8,128)(2,1)S(1)}, u32[]{:S(2)}, u32[]{:S(2)}) async-start(bf16[2,4,2,128,256]{4,3,2,0,1:T(8,128)(2,1)} %copy.85), calls=%async_computation | async-start | bytes 2097152 | tf_op jit(solution)/shard_map/all_to_all | solution.py:127
  44.1 0.0 copy-done.2
  44.1 52.5 %all-to-all-done = bf16[2,4,2,128,256]{4,3,2,0,1:T(8,128)(2,1)S(1)} async-done(((bf16[2,4,2,128,256]{4,3,2,0,1:T(8,128)(2,1)}), bf16[2,4,2,128,256]{4,3,2,0,1:T(8,128)(2,1)S(1)}, u32[]{:S(2)}, u32[]{:S(2)}) %all-to-all-start) | async-done | bytes 1048608 | tf_op jit(solution)/shard_map/all_to_all | solution.py:127
  96.6 1.0 copy.86
  97.6 6.3 %all-gather.3.cloned.1.call-done = f32[64,8192]{1,0:T(8,128)} async-done(((f32[16,8192]{1,0:T(8,128)}), f32[64,8192]{1,0:T(8,128)}) %all-gather.3.cloned.1.call-update) | async-done | bytes 2097168 | tf_op jit(solution)/shard_map/all_gather | solution.py:132
  103.9 1.8 %reduce_sum.86 = f32[16,8192]{1,0:T(8,128)S(1)} reduce(f32[4,16,8192]{2,1,0:T(8,128)} %bitcast.74, f32[]{:T(128)} %constant.13.clone.1), dimensions={0}, to_apply=%region_8.9 | reduce | flops 393216 | bytes 2621444 | tf_op jit(solution)/shard_map/reduce_sum | solution.py:133
  105.7 0.0 copy-done.1
  105.7 0.2 multiply_reduce_fusion
  105.9 0.9 multiply_convert_fusion
  (15 shorter events, 0.2 us)
Async XLA Ops:
  7.2 28.7 %copy-start = (bf16[1,1,8,128,256]{4,3,2,1,0:T(8,128)(2,1)S(1)}, bf16[1,1,8,128,256]{4,3,2,1,0:T(8,128)(2,1)}, u32[]{:S(2)}) copy-start(bf16[1,1,8,128,256]{4,3,2,1,0:T(8,128)(2,1)} %param.20) | copy-start | bytes 1572868
  7.2 96.7 %all-gather.3.cloned.1.call-start = ((), (), s32[]{:S(2)}) async-start(), calls=%async_computation.1 | async-start | bytes 2621440 | tf_op jit(solution)/shard_map/all_gather | solution.py:132
  19.9 13.7 %copy-start.3 = (s32[1,1,8,1]{2,3,1,0:T(1,128)S(1)}, s32[1,1,8,1]{2,3,1,0:T(1,128)}, u32[]{:S(2)}) copy-start(s32[1,1,8,1]{2,3,1,0:T(1,128)} %param.21) | copy-start | bytes 100
  33.6 10.5 %copy-start.2 = (bf16[8192]{0:T(1024)(128)(2,1)S(1)}, bf16[8192]{0:T(1024)(128)(2,1)}, u32[]{:S(2)}) copy-start(bf16[8192]{0:T(1024)(128)(2,1)} %param.19) | copy-start | bytes 49156
  35.9 69.8 %copy-start.1 = (bf16[16,8192]{1,0:T(8,128)(2,1)S(1)}, bf16[16,8192]{1,0:T(8,128)(2,1)}, u32[]{:S(2)}) copy-start(bf16[16,8192]{1,0:T(8,128)(2,1)} %param.17) | copy-start | bytes 786436
  37.7 58.9 %all-to-all-start = ((bf16[2,4,2,128,256]{4,3,2,0,1:T(8,128)(2,1)}), bf16[2,4,2,128,256]{4,3,2,0,1:T(8,128)(2,1)S(1)}, u32[]{:S(2)}, u32[]{:S(2)}) async-start(bf16[2,4,2,128,256]{4,3,2,0,1:T(8,128)(2,1)} %copy.85), calls=%async_computation | async-start | bytes 2097152 | tf_op jit(solution)/shard_map/all_to_all | solution.py:127
Sparse Core Ops, SparseCore 0:
  33.7 70.1 all-gather.2
